TPU v7x, 32 devices: a whole 2x2x4 slice. The times are simulated.
32 devices in a mesh: grp: 2 (over y), row: 8 (over z, x), col: 1, ch: 2 (over core).
Axes of the slice: x: 2, y: 2, z: 4, core: 2. Of those that a mesh axis runs over, the one named last changes fastest.
Arguments:
- pair_act: bfloat16 [128, 256, 128], P('ch', ('grp', 'row'), 'col'), parts along dimension 1, may hold values from -48 to 48
- in_gain: float32 [128], P('ch'), may hold values from 0.1 to 1.9
- left_proj: bfloat16 [128, 128], P(None, 'ch'), may hold values from -0.5 to 0.5
- left_gate: bfloat16 [128, 128], P(None, 'ch'), may hold values from -0.5 to 0.5
- right_proj: bfloat16 [128, 128], P(None, 'ch'), may hold values from -0.5 to 0.5
- right_gate: bfloat16 [128, 128], P(None, 'ch'), may hold values from -0.5 to 0.5
- out_gate: bfloat16 [128, 128], P(None, 'ch'), may hold values from -0.5 to 0.5
- out_gain: float32 [128], P('ch'), may hold values from 0.1 to 1.9
- out_proj: bfloat16 [128, 128], P(None, 'ch'), may hold values from -0.5 to 0.5
Outputs:
- update: bfloat16 [128, 256, 128], P('ch', ('grp', 'row'), 'col'), parts along dimension 1
There are 2 independent parts, one for each index of `grp`. A program takes and returns all parts, laid end to end along the dimension named above; an argument that names none is the same for every part. Nothing has to cross between parts.
All inputs are finite; a program needn't handle non-finite values.
Results may differ from a plain program's by a relative error of at most 0.0085.
Values may be sent and summed in bfloat16 or wider, within the bound.
A program may use at most 64 MiB of HBM per device.

v0:
```python
import jax
import jax.numpy as jnp
from jax import lax
from jax.sharding import PartitionSpec as P


def spread_2(value, axis, source):
    kept = jnp.where(lax.axis_index(axis) == source, value, 0).astype(value.dtype)
    return lax.psum(kept, axis)


def moments(values, channel_count):
    first_sums, squares = lax.psum(
        (jnp.sum(values, axis=0), jnp.sum(values * values, axis=0)), "ch"
    )
    average = first_sums / channel_count
    spread = squares / channel_count - average * average
    centred = values - average[None]
    return centred * lax.rsqrt(spread + 1e-05)[None]


def per_device(
    pair_act, in_gain, left_proj, left_gate, right_proj, right_gate, out_gate, out_gain, out_proj
):
    row_count = pair_act.shape[1]
    col_count = pair_act.shape[2]
    hidden = left_proj.shape[1]
    fan_out = col_count // row_count
    normed = (
        moments(pair_act.astype(jnp.float32), pair_act.shape[0] * lax.axis_size("ch"))
        * in_gain[:, None, None]
    ).astype(jnp.bfloat16)
    whole = lax.all_gather(normed, "ch", axis=0, tiled=True)
    left_weights = jnp.concatenate((left_proj, left_gate), axis=1)
    left_lifted = jnp.einsum("cxy,cn->nyx", whole, left_weights, preferred_element_type=jnp.float32)
    left_edge = (jax.nn.sigmoid(left_lifted[hidden:]) * left_lifted[:hidden]).astype(jnp.bfloat16)
    other_weights = jnp.concatenate((right_proj, right_gate, out_gate), axis=1)
    other_lifted = jnp.einsum(
        "cxy,cn->nxy", whole, other_weights, preferred_element_type=jnp.float32
    )
    right_edge = (jax.nn.sigmoid(other_lifted[hidden : 2 * hidden]) * other_lifted[:hidden]).astype(
        jnp.bfloat16
    )
    gate_map = jax.nn.sigmoid(other_lifted[2 * hidden :])
    blocks = left_edge.reshape(hidden, fan_out, row_count, row_count)
    outgoing = jnp.tile(blocks, (1, lax.axis_size("row") // fan_out, 1, 1))
    arrived = lax.all_to_all(outgoing, "row", split_axis=1, concat_axis=3, tiled=True)
    left_panel = arrived.reshape(hidden, row_count, -1)
    left_panel = spread_2(left_panel, "col", lax.axis_index("row") // fan_out)
    tri_sum = jnp.einsum(
        "hik,hkj->hij",
        left_panel,
        lax.all_gather(right_edge, "row", axis=1, tiled=True),
        preferred_element_type=jnp.float32,
    )
    mid_norm = (moments(tri_sum, hidden * lax.axis_size("ch")) * out_gain[:, None, None]).astype(
        jnp.bfloat16
    )
    all_mid = lax.all_gather(mid_norm, "ch", axis=0, tiled=True)
    projected = jnp.einsum("hxy,hc->cxy", all_mid, out_proj, preferred_element_type=jnp.float32)
    return (gate_map * projected).astype(jnp.bfloat16)


def solution(mesh):
    return jax.shard_map(
        per_device,
        mesh=mesh,
        in_specs=(
            P("ch", ("grp", "row"), "col"),
            P("ch"),
            P(None, "ch"),
            P(None, "ch"),
            P(None, "ch"),
            P(None, "ch"),
            P(None, "ch"),
            P("ch"),
            P(None, "ch"),
        ),
        out_specs=P("ch", ("grp", "row"), "col"),
        check_vma=False,
    )
```

profile of v0, /device:TPU:0, one launch (start us, length us, event | category | flops | bytes accessed | tf_op | source)
XLA Modules:
  0.0 88.3 jit_solution(10436490548046105974)
XLA Ops:
  6.5 0.0 copy-start
  6.5 0.0 all-gather.2.cloned.1.call-start
  6.5 1.1 %convert_reduce_fusion = (f32[16,128]{1,0:T(8,128)S(1)}, f32[16,128]{1,0:T(8,128)S(1)}) fusion(bf16[64,16,128]{2,1,0:T(8,128)(2,1)} %param.9), kind=kLoop, calls=%fused_computation.8 | loop fusion | flops 520192 | bytes 278528 | tf_op jit(solution)/shard_map/reduce_sum | solution.py:14
  7.6 3.6 %all-reduce.1 = (f32[16,128]{1,0:T(8,128)S(1)}, f32[16,128]{1,0:T(8,128)S(1)}) all-reduce(f32[16,128]{1,0:T(8,128)S(1)} %get-tuple-element.8, f32[16,128]{1,0:T(8,128)S(1)} %get-tuple-element.7), channel_id=1, replica_groups=mesh['grp'=2,'row'=8,'col'=1,'ch'=2] {'ch'}, use_global_device_ids=true, to_apply=%region_3.0 | all-reduce | flops 4096 | bytes 32768 | tf_op jit(solution)/shard_map/psum | solution.py:13
  11.2 1.1 %fusion.6 = bf16[64,16,128]{2,0,1:T(8,128)(2,1)S(1)} fusion(f32[64]{0:T(128)} %param.10, f32[16,128]{1,0:T(8,128)S(1)} %get-tuple-element.16, f32[16,128]{1,0:T(8,128)S(1)} %get-tuple-element.15, bf16[64,16,128]{2,1,0:T(8,128)(2,1)} %param.9), kind=kLoop, calls=%fused_computation.11 | loop fusion | flops 655360 | bytes 540928 | tf_op jit(solution)/shard_map/convert_element_type | solution.py:32
  12.3 0.0 copy-start.1
  12.4 0.0 copy-start.2
  12.4 2.2 %all_gather.9 = bf16[128,16,128]{2,0,1:T(8,128)(2,1)S(1)} all-gather(bf16[64,16,128]{2,0,1:T(8,128)(2,1)S(1)} %fusion.6), channel_id=1, replica_groups=mesh['grp'=2,'row'=8,'col'=1,'ch'=2] {'ch'}, dimensions={0}, use_global_device_ids=true | all-gather | bytes 786432 | tf_op jit(solution)/shard_map/all_gather | solution.py:33
  14.5 1.1 %fusion.20 = f32[192,16,128]{2,0,1:T(8,128)S(1)} fusion(bf16[128,16,128]{2,0,1:T(8,128)(2,1)S(1)} %all_gather.9, bf16[128,64]{0,1:T(8,128)(2,1)} %param.15, bf16[128,64]{0,1:T(8,128)(2,1)} %param.14, bf16[128,64]{0,1:T(8,128)(2,1)} %param.13), kind=kOutput, calls=%fused_computation.34 | convolution fusion | flops 100810752 | bytes 2146304 | tf_op jit(solution)/shard_map/cxy,cn->nxy/dot_general | solution.py:38
  15.6 0.9 fusion.8
  16.5 0.0 all-gather.2.cloned.1.call-update
  16.5 0.0 copy-done.1
  16.6 0.0 copy-done.2
  16.6 0.3 convolution_bitcast_fusion
  16.9 0.1 fusion.12
  17.0 0.4 copy.23
  17.4 1.1 %reshape.17 = bf16[8,2,8192]{2,1,0:T(2,128)(2,1)} reshape(bf16[8,16,16,64]{3,2,1,0:T(8,128)(2,1)S(1)} %bitcast.29) | data formatting | bytes 524288
  18.5 7.0 %all-to-all-start = ((bf16[8,2,8192]{2,1,0:T(2,128)(2,1)}), bf16[8,2,8192]{2,1,0:T(2,128)(2,1)S(1)}, u32[]{:S(2)}, u32[]{:S(2)}) async-start(bf16[8,2,8192]{2,1,0:T(2,128)(2,1)} %reshape.17), calls=%async_computation | async-start | bytes 524288 | tf_op jit(solution)/shard_map/all_to_all | solution.py:47
  25.5 14.5 %all-to-all-done = bf16[8,2,8192]{2,1,0:T(2,128)(2,1)S(1)} async-done(((bf16[8,2,8192]{2,1,0:T(2,128)(2,1)}), bf16[8,2,8192]{2,1,0:T(2,128)(2,1)S(1)}, u32[]{:S(2)}, u32[]{:S(2)}) %all-to-all-start) | async-done | bytes 262176 | tf_op jit(solution)/shard_map/all_to_all | solution.py:47
  40.0 0.3 reshape.18
  40.5 0.0 copy-start.3
  40.5 0.3 copy.25
  40.8 30.4 %all-gather.2.cloned.1.call-done = bf16[64,128,128]{2,0,1:T(8,128)(2,1)} async-done(((bf16[64,16,128]{2,0,1:T(8,128)(2,1)}), bf16[64,128,128]{2,0,1:T(8,128)(2,1)}) %all-gather.2.cloned.1.call-update) | async-done | bytes 2097168 | tf_op jit(solution)/shard_map/all_gather | solution.py:53
  71.2 3.5 %fusion.30 = (f32[16,128]{1,0:T(8,128)S(1)}, f32[16,128]{1,0:T(8,128)S(1)}, f32[64,16,128]{2,1,0:T(8,128)S(1)}) fusion(bf16[64,16,128]{2,1,0:T(8,128)(2,1)S(1)} %copy.25, bf16[64,128,128]{2,0,1:T(8,128)(2,1)} %all-gather.2.cloned.1.call-done), kind=kOutput, calls=%fused_computation.49 | convolution fusion | flops 33943552 | bytes 2899968 | tf_op jit(solution)/shard_map/hik,hkj->hij/dot_general | solution.py:50
  74.6 3.3 %all-reduce = (f32[16,128]{1,0:T(8,128)S(1)}, f32[16,128]{1,0:T(8,128)S(1)}) all-reduce(f32[16,128]{1,0:T(8,128)S(1)} %get-tuple-element.6, f32[16,128]{1,0:T(8,128)S(1)} %get-tuple-element.5), channel_id=1, replica_groups=mesh['grp'=2,'row'=8,'col'=1,'ch'=2] {'ch'}, use_global_device_ids=true, to_apply=%region_7.8 | all-reduce | flops 4096 | bytes 32768 | tf_op jit(solution)/shard_map/psum | solution.py:13
  77.9 0.0 copy-done.3
  78.0 0.1 multiply_convert_fusion
  78.1 2.2 %all_gather.11 = bf16[128,16,128]{2,1,0:T(8,128)(2,1)S(1)} all-gather(bf16[64,16,128]{2,1,0:T(8,128)(2,1)S(1)} %multiply_convert_fusion), channel_id=1, replica_groups=mesh['grp'=2,'row'=8,'col'=1,'ch'=2] {'ch'}, dimensions={0}, use_global_device_ids=true | all-gather | bytes 786432 | tf_op jit(solution)/shard_map/all_gather | solution.py:59
  80.3 0.0 copy-done
  80.3 0.3 fusion.3
  80.5 0.9 copy.28
  (4 shorter events, 0.1 us)
Async XLA Ops:
  6.5 73.8 %copy-start = (bf16[128,64]{0,1:T(8,128)(2,1)S(1)}, bf16[128,64]{0,1:T(8,128)(2,1)}, u32[]{:S(2)}) copy-start(bf16[128,64]{0,1:T(8,128)(2,1)} %param.17) | copy-start | bytes 49156
  6.5 64.7 %all-gather.2.cloned.1.call-start = ((), (), s32[]{:S(2)}) async-start(), calls=%async_computation.1 | async-start | bytes 2359296 | tf_op jit(solution)/shard_map/all_gather | solution.py:53
  12.3 4.2 %copy-start.1 = (bf16[128,64]{0,1:T(8,128)(2,1)S(1)}, bf16[128,64]{0,1:T(8,128)(2,1)}, u32[]{:S(2)}) copy-start(bf16[128,64]{0,1:T(8,128)(2,1)} %param.12) | copy-start | bytes 49156
  12.4 4.2 %copy-start.2 = (bf16[128,64]{0,1:T(8,128)(2,1)S(1)}, bf16[128,64]{0,1:T(8,128)(2,1)}, u32[]{:S(2)}) copy-start(bf16[128,64]{0,1:T(8,128)(2,1)} %param.11) | copy-start | bytes 49156
  18.5 21.5 %all-to-all-start = ((bf16[8,2,8192]{2,1,0:T(2,128)(2,1)}), bf16[8,2,8192]{2,1,0:T(2,128)(2,1)S(1)}, u32[]{:S(2)}, u32[]{:S(2)}) async-start(bf16[8,2,8192]{2,1,0:T(2,128)(2,1)} %reshape.17), calls=%async_computation | async-start | bytes 524288 | tf_op jit(solution)/shard_map/all_to_all | solution.py:47
  40.5 37.5 %copy-start.3 = (f32[64]{0:T(128)S(1)}, f32[64]{0:T(128)}, u32[]{:S(2)}) copy-start(f32[64]{0:T(128)} %param.16) | copy-start | bytes 772
Sparse Core Ops, SparseCore 0:
  16.7 54.4 all-gather.1
where the time goes:
time: 88.7 us; the launch traced here: 88.3 us
  waiting for transfers between devices  45 us (51%)
  between operations  13.5 us (15%)
  blocking collectives  11.3 us (13%)
  starting transfers between devices  6.96 us (8%)
  matrix products  5.09 us (6%)
  other arithmetic  3.38 us (4%)
  local copies, waits for them, and re-layouts  3.09 us (3%)
    all_gather x1, waiting for transfers between devices, per_device(): lax.all_gather(right_edge, 'row', axis=1, tiled=True)  30.4 us
    all_to_all x1, waiting for transfers between devices, per_device(): lax.all_to_all(outgoing, 'row', split_axis=1, concat_axis=3, tiled=True)  14.5 us
    all_to_all x1, starting transfers between devices, per_device(): lax.all_to_all(outgoing, 'row', split_axis=1, concat_axis=3, tiled=True)  6.96 us
    psum x2, blocking collectives, moments(): lax.psum((jnp.sum(values, axis=0), jnp.sum(values * values, axis=0)), 'ch')  6.9 us
    dot_general x1, matrix products, per_device(): jnp.einsum('hik,hkj->hij', left_panel, lax.all_gather(right_edge, 'row',...  3.46 us
    all_gather x1, blocking collectives, per_device(): whole = lax.all_gather(normed, 'ch', axis=0, tiled=True)  2.18 us
    all_gather x1, blocking collectives, per_device(): all_mid = lax.all_gather(mid_norm, 'ch', axis=0, tiled=True)  2.18 us
  transfers between devices with their start and end apart: 2, of which 2 were waited for; matrix products, arithmetic and copies ran while one was open for 3% of the time, Pallas kernels for 0%

commit v1 on v0

--- a/solution.py
+++ b/solution.py
@@ -2,6 +2,22 @@
 import jax.numpy as jnp
 from jax import lax
 from jax.sharding import PartitionSpec as P
+
+
+def product_in_turn(x, axis, dim, product):
+    size, here, rows = (lax.axis_size(axis), lax.axis_index(axis), x.shape[dim])
+    right = [(i, (i + 1) % size) for i in range(size)]
+    left = [(i, (i - 1) % size) for i in range(size)]
+    half = size // 2
+    from_left = from_right = x
+    total = product(x, here * rows)
+    for step in range(1, half + 1):
+        from_left = lax.ppermute(from_left, axis, right)
+        if step < size - half:
+            from_right = lax.ppermute(from_right, axis, left)
+            total = total + product(from_right, (here + step) % size * rows)
+        total = total + product(from_left, (here - step) % size * rows)
+    return total
 
 
 def spread_2(value, axis, source):
@@ -47,11 +63,16 @@
     arrived = lax.all_to_all(outgoing, "row", split_axis=1, concat_axis=3, tiled=True)
     left_panel = arrived.reshape(hidden, row_count, -1)
     left_panel = spread_2(left_panel, "col", lax.axis_index("row") // fan_out)
-    tri_sum = jnp.einsum(
-        "hik,hkj->hij",
-        left_panel,
-        lax.all_gather(right_edge, "row", axis=1, tiled=True),
-        preferred_element_type=jnp.float32,
+    tri_sum = product_in_turn(
+        right_edge,
+        "row",
+        1,
+        lambda shard, at: jnp.einsum(
+            "hik,hkj->hij",
+            lax.dynamic_slice_in_dim(left_panel, at, shard.shape[1], axis=2),
+            shard,
+            preferred_element_type=jnp.float32,
+        ),
     )
     mid_norm = (moments(tri_sum, hidden * lax.axis_size("ch")) * out_gain[:, None, None]).astype(
         jnp.bfloat16

time: 88.7 us -> 75.7 us (0.85)
  waiting for transfers between devices: 45 us -> 24.5 us
  starting transfers between devices: 6.96 us -> 23.7 us
  between operations: 13.5 us -> 0.28 us
  local copies, waits for them, and re-layouts: 3.09 us -> 5.64 us
  matrix products: 5.09 us -> 7.22 us
    all_gather x1 -> x0, waiting for transfers between devices: 30.4 us -> none  [per_device(): lax.all_gather(right_edge, 'row', axis=1, tiled=True)]
    ppermute x0 -> x7, waiting for transfers between devices: none -> 24.5 us  [the longest x4 24.5 us: product_in_turn(): from_left = lax.ppermute(from_left, axis, right)]
    ppermute x0 -> x7, starting transfers between devices: none -> 16.7 us  [the longest x4 9.49 us: product_in_turn(): from_left = lax.ppermute(from_left, axis, right)]
    all_to_all x1, waiting for transfers between devices: 14.5 us -> 0.01 us  [per_device(): lax.all_to_all(outgoing, 'row', split_axis=1, concat_axis=3, tiled=True)]
    dot_general x1 -> x8, matrix products: 3.46 us -> 6.33 us  [per_device(): jnp.einsum('hik,hkj->hij', lax.dynamic_slice_in_dim(left_panel, at, shard...]
    unnamed x10 -> x26, local copies, waits for them, and re-layouts: 1.46 us -> 4.2 us
  transfers between devices with their start and end apart: 2 -> 8, of which waited for: 2 -> 4; matrix products, arithmetic and copies ran while one was open for 3% -> 13% of each run, Pallas kernels for 0% -> 0%
where the time goes in v1:
time: 75.7 us; the launch traced here: 75.3 us
  waiting for transfers between devices  24.5 us (32%)
  starting transfers between devices  23.7 us (31%)
  blocking collectives  11.3 us (15%)
  matrix products  7.22 us (10%)
  local copies, waits for them, and re-layouts  5.64 us (7%)
  other arithmetic  2.68 us (4%)
    ppermute x4, waiting for transfers between devices, product_in_turn(): from_left = lax.ppermute(from_left, axis, right)  24.5 us
    ppermute x4, starting transfers between devices, product_in_turn(): from_left = lax.ppermute(from_left, axis, right)  9.49 us
    ppermute x3, starting transfers between devices, product_in_turn(): from_right = lax.ppermute(from_right, axis, left)  7.21 us
    all_to_all x1, starting transfers between devices, per_device(): lax.all_to_all(outgoing, 'row', split_axis=1, concat_axis=3, tiled=True)  6.96 us
    psum x2, blocking collectives, moments(): lax.psum((jnp.sum(values, axis=0), jnp.sum(values * values, axis=0)), 'ch')  6.91 us
    dot_general x8, matrix products, per_device(): jnp.einsum('hik,hkj->hij', lax.dynamic_slice_in_dim(left_panel, at, shard...  6.33 us
    unnamed x26, local copies, waits for them, and re-layouts  4.2 us
    all_gather x1, blocking collectives, per_device(): whole = lax.all_gather(normed, 'ch', axis=0, tiled=True)  2.18 us
  transfers between devices with their start and end apart: 8, of which 4 were waited for; matrix products, arithmetic and copies ran while one was open for 13% of the time, Pallas kernels for 0%

profile of v1, /device:TPU:0, one launch (start us, length us, event | category | flops | bytes accessed | tf_op | source)
XLA Modules:
  0.0 75.3 jit_solution(17997379783592150171)
XLA Ops:
  0.0 1.1 %convert_reduce_fusion = (f32[16,128]{1,0:T(8,128)S(1)}, f32[16,128]{1,0:T(8,128)S(1)}) fusion(bf16[64,16,128]{2,1,0:T(8,128)(2,1)} %param.9), kind=kLoop, calls=%fused_computation.13 | loop fusion | flops 520192 | bytes 278528 | tf_op jit(solution)/shard_map/reduce_sum | solution.py:30
  1.1 3.6 %all-reduce.1 = (f32[16,128]{1,0:T(8,128)S(1)}, f32[16,128]{1,0:T(8,128)S(1)}) all-reduce(f32[16,128]{1,0:T(8,128)S(1)} %get-tuple-element.8, f32[16,128]{1,0:T(8,128)S(1)} %get-tuple-element.7), channel_id=1, replica_groups=mesh['grp'=2,'row'=8,'col'=1,'ch'=2] {'ch'}, use_global_device_ids=true, to_apply=%region_3.0 | all-reduce | flops 4096 | bytes 32768 | tf_op jit(solution)/shard_map/psum | solution.py:29
  4.7 1.1 %fusion.6 = bf16[64,16,128]{2,0,1:T(8,128)(2,1)S(1)} fusion(f32[64]{0:T(128)} %param.10, f32[16,128]{1,0:T(8,128)S(1)} %get-tuple-element.24, f32[16,128]{1,0:T(8,128)S(1)} %get-tuple-element.23, bf16[64,16,128]{2,1,0:T(8,128)(2,1)} %param.9), kind=kLoop, calls=%fused_computation.16 | loop fusion | flops 655360 | bytes 540928 | tf_op jit(solution)/shard_map/convert_element_type | solution.py:48
  5.8 2.2 %all_gather.6 = bf16[128,16,128]{2,0,1:T(8,128)(2,1)S(1)} all-gather(bf16[64,16,128]{2,0,1:T(8,128)(2,1)S(1)} %fusion.6), channel_id=1, replica_groups=mesh['grp'=2,'row'=8,'col'=1,'ch'=2] {'ch'}, dimensions={0}, use_global_device_ids=true | all-gather | bytes 786432 | tf_op jit(solution)/shard_map/all_gather | solution.py:49
  8.0 0.3 convolution_bitcast_fusion
  8.3 0.0 copy-start.4
  8.3 0.0 copy-start.5
  8.3 0.1 fusion.12
  8.5 0.4 copy.44
  8.9 1.1 %reshape.17 = bf16[8,2,8192]{2,1,0:T(2,128)(2,1)} reshape(bf16[8,16,16,64]{3,2,1,0:T(8,128)(2,1)S(1)} %bitcast.36) | data formatting | bytes 524288
  10.0 7.0 %all-to-all-start = ((bf16[8,2,8192]{2,1,0:T(2,128)(2,1)}), bf16[8,2,8192]{2,1,0:T(2,128)(2,1)S(1)}, u32[]{:S(2)}, u32[]{:S(2)}) async-start(bf16[8,2,8192]{2,1,0:T(2,128)(2,1)} %reshape.17), calls=%async_computation | async-start | bytes 524288 | tf_op jit(solution)/shard_map/all_to_all | solution.py:63
  17.0 0.4 fusion.31
  17.4 0.1 fusion.8
  17.5 2.1 %collective-permute-start.1 = (bf16[64,16,128]{2,0,1:T(8,128)(2,1)S(1)}, bf16[64,16,128]{2,0,1:T(8,128)(2,1)}, u32[]{:S(2)}, u32[]{:S(2)}) collective-permute-start(bf16[64,16,128]{2,0,1:T(8,128)(2,1)S(1)} %fusion.8), channel_id=1, source_target_pairs={{0,2},{2,4},{4,6},{6,8},{8,10},{10,12},{12,14},{14,0},{1,3},{3,5},... | collective-permute-start | bytes 786440 | tf_op jit(solution)/shard_map/ppermute | solution.py:15
  19.6 2.8 %collective-permute-start = (bf16[64,16,128]{2,0,1:T(8,128)(2,1)S(1)}, bf16[64,16,128]{2,0,1:T(8,128)(2,1)}, u32[]{:S(2)}, u32[]{:S(2)}) collective-permute-start(bf16[64,16,128]{2,0,1:T(8,128)(2,1)S(1)} %fusion.8), channel_id=1, source_target_pairs={{0,14},{2,0},{4,2},{6,4},{8,6},{10,8},{12,10},{14,12},{1,15},{3,1}... | collective-permute-start | bytes 786440 | tf_op jit(solution)/shard_map/ppermute | solution.py:17
  22.4 10.1 %collective-permute-done.1 = bf16[64,16,128]{2,0,1:T(8,128)(2,1)} collective-permute-done((bf16[64,16,128]{2,0,1:T(8,128)(2,1)S(1)}, bf16[64,16,128]{2,0,1:T(8,128)(2,1)}, u32[]{:S(2)}, u32[]{:S(2)}) %collective-permute-start.1) | collective-permute-done | bytes 262176 | tf_op jit(solution)/shard_map/ppermute | solution.py:15
  32.5 2.6 %collective-permute-start.3 = (bf16[64,16,128]{2,0,1:T(8,128)(2,1)}, bf16[64,16,128]{2,0,1:T(8,128)(2,1)}, u32[]{:S(2)}, u32[]{:S(2)}) collective-permute-start(bf16[64,16,128]{2,0,1:T(8,128)(2,1)} %collective-permute-done.1), channel_id=1, source_target_pairs={{0,2},{2,4},{4,6},{6,8},{8,10},{10,12},{12,14},{14,0},{1,3},{3,5},... | collective-permute-start | bytes 786440 | tf_op jit(solution)/shard_map/ppermute | solution.py:15
  35.1 2.1 %collective-permute-start.2 = (bf16[64,16,128]{2,0,1:T(8,128)(2,1)}, bf16[64,16,128]{2,0,1:T(8,128)(2,1)}, u32[]{:S(2)}, u32[]{:S(2)}) collective-permute-start(bf16[64,16,128]{2,0,1:T(8,128)(2,1)} %collective-permute-done), channel_id=1, source_target_pairs={{0,14},{2,0},{4,2},{6,4},{8,6},{10,8},{12,10},{14,12},{1,15},{3,1}... | collective-permute-start | bytes 786440 | tf_op jit(solution)/shard_map/ppermute | solution.py:17
  37.2 0.3 reshape.18
  37.7 0.1 constant_dynamic-slice_fusion
  37.8 0.3 copy.64
  38.0 0.3 fusion.29
  38.3 0.3 copy.65
  38.6 0.3 copy.66
  38.9 1.3 %convolution_add_fusion.4 = f32[64,16,128]{2,1,0:T(8,128)S(1)} fusion(f32[64,16,128]{2,1,0:T(8,128)S(1)} %fusion.29, bf16[64,16,16]{2,1,0:T(8,128)(2,1)S(1)} %copy.65, bf16[64,16,128]{2,0,1:T(8,128)(2,1)} %collective-permute-done), kind=kOutput, calls=%fused_computation.9 | convolution fusion | flops 4325376 | bytes 1343488 | tf_op jit(solution)/shard_map/hik,hkj->hij/dot_general | solution.py:70
  40.1 1.3 %convolution_add_fusion.3 = f32[64,16,128]{2,1,0:T(8,128)S(1)} fusion(f32[64,16,128]{2,1,0:T(8,128)S(1)} %convolution_add_fusion.4, bf16[64,16,16]{2,1,0:T(8,128)(2,1)S(1)} %copy.66, bf16[64,16,128]{2,0,1:T(8,128)(2,1)} %collective-permute-done.1), kind=kOutput, calls=%fused_computation.8 | convolution fusion | flops 4325376 | bytes 1343488 | tf_op jit(solution)/shard_map/hik,hkj->hij/dot_general | solution.py:70
  41.4 0.3 copy.68
  41.6 0.3 copy.67
  41.9 0.3 copy.70
  42.2 0.9 %copy.69 = bf16[64,16,16]{2,1,0:T(8,128)(2,1)} copy(bf16[64,16,16]{0,2,1:T(8,128)(2,1)S(1)} %get-tuple-element.15) | data formatting | bytes 65536
  43.1 0.2 copy.71
  43.4 2.9 %collective-permute-done.3 = bf16[64,16,128]{2,0,1:T(8,128)(2,1)} collective-permute-done((bf16[64,16,128]{2,0,1:T(8,128)(2,1)}, bf16[64,16,128]{2,0,1:T(8,128)(2,1)}, u32[]{:S(2)}, u32[]{:S(2)}) %collective-permute-start.3) | collective-permute-done | bytes 262176 | tf_op jit(solution)/shard_map/ppermute | solution.py:15
  46.2 2.5 %collective-permute-start.5 = (bf16[64,16,128]{2,0,1:T(8,128)(2,1)}, bf16[64,16,128]{2,0,1:T(8,128)(2,1)S(1)}, u32[]{:S(2)}, u32[]{:S(2)}) collective-permute-start(bf16[64,16,128]{2,0,1:T(8,128)(2,1)} %collective-permute-done.3), channel_id=1, source_target_pairs={{0,2},{2,4},{4,6},{6,8},{8,10},{10,12},{12,14},{14,0},{1,3},{3,5},... | collective-permute-start | bytes 786440 | tf_op jit(solution)/shard_map/ppermute | solution.py:15
  48.7 1.3 %fusion.24 = f32[64,16,128]{2,1,0:T(8,128)S(1)} fusion(bf16[64,16,16]{2,1,0:T(8,128)(2,1)S(1)} %copy.68, bf16[64,16,128]{2,0,1:T(8,128)(2,1)} %collective-permute-done.3), kind=kOutput, calls=%fused_computation.42 | convolution fusion | flops 4194304 | bytes 819200 | tf_op jit(solution)/shard_map/hik,hkj->hij/dot_general | solution.py:70
  50.0 2.3 %collective-permute-start.4 = (bf16[64,16,128]{2,0,1:T(8,128)(2,1)}, bf16[64,16,128]{2,0,1:T(8,128)(2,1)S(1)}, u32[]{:S(2)}, u32[]{:S(2)}) collective-permute-start(bf16[64,16,128]{2,0,1:T(8,128)(2,1)} %collective-permute-done.2), channel_id=1, source_target_pairs={{0,14},{2,0},{4,2},{6,4},{8,6},{10,8},{12,10},{14,12},{1,15},{3,1}... | collective-permute-start | bytes 786440 | tf_op jit(solution)/shard_map/ppermute | solution.py:17
  52.3 1.3 %fusion.2 = f32[64,16,128]{2,1,0:T(8,128)S(1)} fusion(f32[64,16,128]{2,1,0:T(8,128)S(1)} %fusion.24, f32[64,16,128]{2,1,0:T(8,128)S(1)} %convolution_add_fusion.3, bf16[64,16,16]{2,1,0:T(8,128)(2,1)S(1)} %copy.67, bf16[64,16,128]{2,0,1:T(8,128)(2,1)} %collective-permute-done.2), kind=kOutput, calls=%fused_computation.7 | convolution fusion | flops 4456448 | bytes 1867776 | tf_op jit(solution)/shard_map/hik,hkj->hij/dot_general | solution.py:70
  53.6 5.5 %collective-permute-done.5 = bf16[64,16,128]{2,0,1:T(8,128)(2,1)S(1)} collective-permute-done((bf16[64,16,128]{2,0,1:T(8,128)(2,1)}, bf16[64,16,128]{2,0,1:T(8,128)(2,1)S(1)}, u32[]{:S(2)}, u32[]{:S(2)}) %collective-permute-start.5) | collective-permute-done | bytes 262176 | tf_op jit(solution)/shard_map/ppermute | solution.py:15
  59.1 2.4 %collective-permute-start.6 = (bf16[64,16,128]{2,0,1:T(8,128)(2,1)S(1)}, bf16[64,16,128]{2,0,1:T(8,128)(2,1)S(1)}, u32[]{:S(2)}, u32[]{:S(2)}) collective-permute-start(bf16[64,16,128]{2,0,1:T(8,128)(2,1)S(1)} %collective-permute-done.5), channel_id=1, source_target_pairs={{0,2},{2,4},{4,6},{6,8},{8,10},{10,12},{12,14},{14,0},{1,3},{3,5},... | collective-permute-start | bytes 786440 | tf_op jit(solution)/shard_map/ppermute | solution.py:15
  61.5 0.3 fusion.21
  61.8 0.0 copy-start.7
  61.8 0.3 fusion.1
  62.1 6.0 %collective-permute-done.6 = bf16[64,16,128]{2,0,1:T(8,128)(2,1)S(1)} collective-permute-done((bf16[64,16,128]{2,0,1:T(8,128)(2,1)S(1)}, bf16[64,16,128]{2,0,1:T(8,128)(2,1)S(1)}, u32[]{:S(2)}, u32[]{:S(2)}) %collective-permute-start.6) | collective-permute-done | bytes 262176 | tf_op jit(solution)/shard_map/ppermute | solution.py:15
  68.1 0.3 fusion.41
  68.5 3.3 %all-reduce = (f32[16,128]{1,0:T(8,128)S(1)}, f32[16,128]{1,0:T(8,128)S(1)}) all-reduce(f32[16,128]{1,0:T(8,128)S(1)} %get-tuple-element.6, f32[16,128]{1,0:T(8,128)S(1)} %get-tuple-element.5), channel_id=1, replica_groups=mesh['grp'=2,'row'=8,'col'=1,'ch'=2] {'ch'}, use_global_device_ids=true, to_apply=%region_7.8 | all-reduce | flops 4096 | bytes 32768 | tf_op jit(solution)/shard_map/psum | solution.py:29
  71.8 0.1 multiply_convert_fusion
  71.9 2.2 %all_gather.7 = bf16[128,16,128]{2,1,0:T(8,128)(2,1)S(1)} all-gather(bf16[64,16,128]{2,1,0:T(8,128)(2,1)S(1)} %multiply_convert_fusion), channel_id=1, replica_groups=mesh['grp'=2,'row'=8,'col'=1,'ch'=2] {'ch'}, dimensions={0}, use_global_device_ids=true | all-gather | bytes 786432 | tf_op jit(solution)/shard_map/all_gather | solution.py:80
  74.1 0.3 fusion.3
  74.4 0.9 %copy.63 = bf16[64,16,128]{2,1,0:T(8,128)(2,1)} copy(bf16[64,16,128]{2,0,1:T(8,128)(2,1)S(1)} %fusion.3) | data formatting | bytes 524288 | tf_op jit(solution)/shard_map/convert_element_type | solution.py:82
  (21 shorter events, 0.1 us)
Async XLA Ops:
  0.0 74.1 %copy-start = (bf16[128,64]{0,1:T(8,128)(2,1)S(1)}, bf16[128,64]{0,1:T(8,128)(2,1)}, u32[]{:S(2)}) copy-start(bf16[128,64]{0,1:T(8,128)(2,1)} %param.17) | copy-start | bytes 49156
  0.0 8.0 %copy-start.3 = (bf16[128,64]{0,1:T(8,128)(2,1)S(1)}, bf16[128,64]{0,1:T(8,128)(2,1)}, u32[]{:S(2)}) copy-start(bf16[128,64]{0,1:T(8,128)(2,1)} %param.11) | copy-start | bytes 49156
  0.0 8.0 %copy-start.2 = (bf16[128,64]{0,1:T(8,128)(2,1)S(1)}, bf16[128,64]{0,1:T(8,128)(2,1)}, u32[]{:S(2)}) copy-start(bf16[128,64]{0,1:T(8,128)(2,1)} %param.12) | copy-start | bytes 49156
  8.3 8.7 %copy-start.4 = (bf16[128,64]{0,1:T(8,128)(2,1)S(1)}, bf16[128,64]{0,1:T(8,128)(2,1)}, u32[]{:S(2)}) copy-start(bf16[128,64]{0,1:T(8,128)(2,1)} %param.15) | copy-start | bytes 49156
  8.3 8.7 %copy-start.5 = (bf16[128,64]{0,1:T(8,128)(2,1)S(1)}, bf16[128,64]{0,1:T(8,128)(2,1)}, u32[]{:S(2)}) copy-start(bf16[128,64]{0,1:T(8,128)(2,1)} %param.14) | copy-start | bytes 49156
  8.3 8.7 %copy-start.6 = (bf16[128,64]{0,1:T(8,128)(2,1)S(1)}, bf16[128,64]{0,1:T(8,128)(2,1)}, u32[]{:S(2)}) copy-start(bf16[128,64]{0,1:T(8,128)(2,1)} %param.13) | copy-start | bytes 49156
  10.0 27.2 %all-to-all-start = ((bf16[8,2,8192]{2,1,0:T(2,128)(2,1)}), bf16[8,2,8192]{2,1,0:T(2,128)(2,1)S(1)}, u32[]{:S(2)}, u32[]{:S(2)}) async-start(bf16[8,2,8192]{2,1,0:T(2,128)(2,1)} %reshape.17), calls=%async_computation | async-start | bytes 524288 | tf_op jit(solution)/shard_map/all_to_all | solution.py:63
  17.5 15.0 %collective-permute-start.1 = (bf16[64,16,128]{2,0,1:T(8,128)(2,1)S(1)}, bf16[64,16,128]{2,0,1:T(8,128)(2,1)}, u32[]{:S(2)}, u32[]{:S(2)}) collective-permute-start(bf16[64,16,128]{2,0,1:T(8,128)(2,1)S(1)} %fusion.8), channel_id=1, source_target_pairs={{0,2},{2,4},{4,6},{6,8},{8,10},{10,12},{12,14},{14,0},{1,3},{3,5},... | collective-permute-start | bytes 786440 | tf_op jit(solution)/shard_map/ppermute | solution.py:15
  19.6 15.5 %collective-permute-start = (bf16[64,16,128]{2,0,1:T(8,128)(2,1)S(1)}, bf16[64,16,128]{2,0,1:T(8,128)(2,1)}, u32[]{:S(2)}, u32[]{:S(2)}) collective-permute-start(bf16[64,16,128]{2,0,1:T(8,128)(2,1)S(1)} %fusion.8), channel_id=1, source_target_pairs={{0,14},{2,0},{4,2},{6,4},{8,6},{10,8},{12,10},{14,12},{1,15},{3,1}... | collective-permute-start | bytes 786440 | tf_op jit(solution)/shard_map/ppermute | solution.py:17
  32.5 13.7 %collective-permute-start.3 = (bf16[64,16,128]{2,0,1:T(8,128)(2,1)}, bf16[64,16,128]{2,0,1:T(8,128)(2,1)}, u32[]{:S(2)}, u32[]{:S(2)}) collective-permute-start(bf16[64,16,128]{2,0,1:T(8,128)(2,1)} %collective-permute-done.1), channel_id=1, source_target_pairs={{0,2},{2,4},{4,6},{6,8},{8,10},{10,12},{12,14},{14,0},{1,3},{3,5},... | collective-permute-start | bytes 786440 | tf_op jit(solution)/shard_map/ppermute | solution.py:15
  35.1 14.9 %collective-permute-start.2 = (bf16[64,16,128]{2,0,1:T(8,128)(2,1)}, bf16[64,16,128]{2,0,1:T(8,128)(2,1)}, u32[]{:S(2)}, u32[]{:S(2)}) collective-permute-start(bf16[64,16,128]{2,0,1:T(8,128)(2,1)} %collective-permute-done), channel_id=1, source_target_pairs={{0,14},{2,0},{4,2},{6,4},{8,6},{10,8},{12,10},{14,12},{1,15},{3,1}... | collective-permute-start | bytes 786440 | tf_op jit(solution)/shard_map/ppermute | solution.py:17
  46.2 12.9 %collective-permute-start.5 = (bf16[64,16,128]{2,0,1:T(8,128)(2,1)}, bf16[64,16,128]{2,0,1:T(8,128)(2,1)S(1)}, u32[]{:S(2)}, u32[]{:S(2)}) collective-permute-start(bf16[64,16,128]{2,0,1:T(8,128)(2,1)} %collective-permute-done.3), channel_id=1, source_target_pairs={{0,2},{2,4},{4,6},{6,8},{8,10},{10,12},{12,14},{14,0},{1,3},{3,5},... | collective-permute-start | bytes 786440 | tf_op jit(solution)/shard_map/ppermute | solution.py:15
  50.0 11.8 %copy-start.1 = (bf16[64,16,16]{2,1,0:T(8,128)(2,1)S(1)}, bf16[64,16,16]{2,1,0:T(8,128)(2,1)}, u32[]{:S(2)}) copy-start(bf16[64,16,16]{2,1,0:T(8,128)(2,1)} %copy.69) | copy-start | bytes 98308
  50.0 11.8 %collective-permute-start.4 = (bf16[64,16,128]{2,0,1:T(8,128)(2,1)}, bf16[64,16,128]{2,0,1:T(8,128)(2,1)S(1)}, u32[]{:S(2)}, u32[]{:S(2)}) collective-permute-start(bf16[64,16,128]{2,0,1:T(8,128)(2,1)} %collective-permute-done.2), channel_id=1, source_target_pairs={{0,14},{2,0},{4,2},{6,4},{8,6},{10,8},{12,10},{14,12},{1,15},{3,1}... | collective-permute-start | bytes 786440 | tf_op jit(solution)/shard_map/ppermute | solution.py:17
  59.1 9.1 %collective-permute-start.6 = (bf16[64,16,128]{2,0,1:T(8,128)(2,1)S(1)}, bf16[64,16,128]{2,0,1:T(8,128)(2,1)S(1)}, u32[]{:S(2)}, u32[]{:S(2)}) collective-permute-start(bf16[64,16,128]{2,0,1:T(8,128)(2,1)S(1)} %collective-permute-done.5), channel_id=1, source_target_pairs={{0,2},{2,4},{4,6},{6,8},{8,10},{10,12},{12,14},{14,0},{1,3},{3,5},... | collective-permute-start | bytes 786440 | tf_op jit(solution)/shard_map/ppermute | solution.py:15
  61.8 10.0 %copy-start.7 = (f32[64]{0:T(128)S(1)}, f32[64]{0:T(128)}, u32[]{:S(2)}) copy-start(f32[64]{0:T(128)} %param.16) | copy-start | bytes 772
